TPU v7x, 32 devices: a whole 2x2x4 slice. The times are simulated.
32 devices in a mesh: angle: 8 (over y, x, core), scan: 4 (over z).
Axes of the slice: x: 2, y: 2, z: 4, core: 2. Of those that a mesh axis runs over, the one named last changes fastest.
Arguments:
- object_slices: float32 [2, 3, 256, 512], P(None, None, 'scan', 'angle'), may hold values from -5 to 5
- probe: float32 [2, 128, 128], replicated, may hold values from -6 to 6
- intensities: float32 [8, 4, 2, 128, 128], P('angle', 'scan'), may hold values from 0.5 to 3.5
- row_offsets: int32 [8, 4, 2], P('angle', 'scan'), may hold values from 0 to 64
- column_starts: int32 [8, 4, 2], P('angle', 'scan'), may hold values from 0 to 320
- slice_shifts: int32 [8, 3], P('angle'), may hold values from 0 to 64
- counts: int32 [8, 4], P('angle', 'scan'), may hold values from 1 to 2, as said below
Outputs:
- object_gradient: float32 [2, 3, 256, 512], P(None, None, 'scan', 'angle')
- probe_gradient: float32 [2, 128, 128], replicated
Inputs may be any that keep to these rules, and one draw needn't show every extreme that they name: `counts`: the largest value 2 occurs in every draw.
All inputs are finite; a program needn't handle non-finite values.
Results may differ from a plain program's by a relative error of at most 0.0003.
Values sent between devices are 32-bit elements; how exact they have to be, the bound alone decides.
A program may use at most 64 MiB of HBM per device.

v0:
```python
from functools import partial
import jax
import jax.numpy as jnp
from jax import lax
from jax.sharding import PartitionSpec as P


def padded(cells, sides, width):
    for axis, dim in sides:
        count = lax.axis_size(axis)
        ends = count - 1
        head = lax.slice_in_dim(cells, 0, width, axis=dim)
        tail = lax.slice_in_dim(cells, cells.shape[dim] - width, cells.shape[dim], axis=dim)
        cells = jnp.concatenate(
            [
                lax.ppermute(tail, axis, [(i, (i + 1) % count) for i in range(ends)]),
                cells,
                lax.ppermute(head, axis, [((i + 1) % count, i) for i in range(ends)]),
            ],
            axis=dim,
        )
    return cells


def propagator(size):
    index = jnp.arange(size, dtype=jnp.int32)
    centred = ((index + size // 2) % size - size // 2).astype(jnp.float32)
    radius = centred[:, None] * centred[:, None] + centred[None, :] * centred[None, :]
    phase = 8.0 * jnp.pi * radius / (size * size)
    return (jnp.cos(phase), jnp.sin(phase))


def tables(size):
    index = jnp.arange(size, dtype=jnp.int32)
    turns = index[:, None] * index[None, :] % size
    phase = 2.0 * jnp.pi * turns.astype(jnp.float32) / size
    scale = 1.0 / jnp.sqrt(jnp.float32(size))
    return (jnp.cos(phase) * scale, jnp.sin(phase) * scale)


def matmul(first, second):
    return jnp.dot(
        first, second, precision=lax.Precision.HIGHEST, preferred_element_type=jnp.float32
    )


def transform(real_part, imag_part, cosine, sine, sign):
    left_re = matmul(cosine, real_part) - sign * matmul(sine, imag_part)
    left_im = matmul(cosine, imag_part) + sign * matmul(sine, real_part)
    right_re = matmul(left_re, cosine) - sign * matmul(left_im, sine)
    right_im = matmul(left_im, cosine) + sign * matmul(left_re, sine)
    return (right_re, right_im)


def local_loss(slab, probe, measured, weight, cosine, sine, kern_re, kern_im):
    wave_re, wave_im = (probe[0], probe[1])
    layers = slab.shape[1]
    for k in range(layers):
        object_re, object_im = (slab[0, k], slab[1, k])
        wave_re, wave_im = (
            wave_re * object_re - wave_im * object_im,
            wave_re * object_im + wave_im * object_re,
        )
        if k + 1 < layers:
            freq_re, freq_im = transform(wave_re, wave_im, cosine, sine, -1.0)
            freq_re, freq_im = (
                freq_re * kern_re - freq_im * kern_im,
                freq_re * kern_im + freq_im * kern_re,
            )
            wave_re, wave_im = transform(freq_re, freq_im, cosine, sine, 1.0)
    far_re, far_im = transform(wave_re, wave_im, cosine, sine, -1.0)
    differ = far_re * far_re + far_im * far_im - measured
    return weight * jnp.sum(differ * differ)


def local(object_slices, probe, intensities, row_offsets, column_starts, slice_shifts, counts):
    band = object_slices.shape[2]
    framed = padded(object_slices, (("scan", 2),), band)
    region = lax.all_gather(framed, "angle", axis=3, tiled=True)
    size = probe.shape[1]
    slots = row_offsets.shape[2]
    layers = region.shape[1]
    angles = lax.axis_size("angle")
    cosine, sine = tables(size)
    kern_re, kern_im = propagator(size)
    shifts = slice_shifts[0]
    zero = jnp.zeros((), jnp.int32)

    def visit(slot, carry):
        gradient_region, gradient_probe = carry
        top = row_offsets[0, 0, slot]
        start = column_starts[0, 0, slot]
        slab = jnp.concatenate(
            [
                lax.dynamic_slice(
                    region, (zero, zero + k, top, start + shifts[k]), (2, 1, size, size)
                )
                for k in range(layers)
            ],
            axis=1,
        )
        weight = jnp.where(slot < counts[0, 0], 0.5 / angles, 0.0).astype(jnp.float32)
        measured = intensities[0, 0, slot]
        scorer = partial(
            local_loss,
            measured=measured,
            weight=weight,
            cosine=cosine,
            sine=sine,
            kern_re=kern_re,
            kern_im=kern_im,
        )
        loss, pull = jax.vjp(scorer, slab, probe)
        slab_grad, probe_grad = pull(jnp.ones_like(loss))
        for k in range(layers):
            place = (zero, zero + k, top, start + shifts[k])
            current = lax.dynamic_slice(gradient_region, place, (2, 1, size, size))
            gradient_region = lax.dynamic_update_slice(
                gradient_region, current + slab_grad[:, k : k + 1], place
            )
        return (gradient_region, gradient_probe + probe_grad)

    start_carry = (jnp.zeros(region.shape, jnp.float32), jnp.zeros(probe.shape, jnp.float32))
    gradient_region, gradient_probe = lax.fori_loop(0, slots, visit, start_carry)
    shared = lax.psum_scatter(gradient_region, "angle", scatter_dimension=3, tiled=True)
    edges = jnp.concatenate([shared[:, :, :band], shared[:, :, 2 * band :]], axis=2)
    rimmed = padded(edges, (("scan", 2),), band)
    object_gradient = shared[:, :, band : 2 * band] + rimmed[:, :, :band] + rimmed[:, :, 3 * band :]
    group_total = lax.psum(gradient_probe, "scan")
    probe_gradient = lax.psum(group_total, "angle")
    return (object_gradient, probe_gradient)


def solution(mesh):
    return jax.shard_map(
        local,
        mesh=mesh,
        in_specs=(
            P(None, None, "scan", "angle"),
            P(),
            P("angle", "scan", None, None, None),
            P("angle", "scan", None),
            P("angle", "scan", None),
            P("angle", None),
            P("angle", "scan"),
        ),
        out_specs=(P(None, None, "scan", "angle"), P()),
        check_vma=False,
    )
```

profile of v0, /device:TPU:0, one launch (start us, length us, event | category | flops | bytes accessed | tf_op | source)
XLA Modules:
  0.0 352.9 jit_solution(17662193562692884179)
XLA Ops:
  8.3 1.3 collective-permute-start.1
  9.6 5.6 %collective-permute-start = (f32[2,3,64,64]{2,0,1,3:T(2,128)S(1)}, f32[2,3,64,64]{2,0,1,3:T(2,128)S(1)}, u32[]{:S(2)}, u32[]{:S(2)}) collective-permute-start(f32[2,3,64,64]{2,0,1,3:T(2,128)S(1)} %copy.25), channel_id=1, source_target_pairs={{0,1},{1,2},{2,3},{4,5},{5,6},{6,7},{8,9},{9,10},{10,11},{12,13},{... | collective-permute-start | bytes 294920 | tf_op jit(solution)/shard_map/ppermute | solution.py:16
  15.2 2.9 collective-permute-done.1
  20.7 34.6 %all-gather.2.cloned.1.call-done = f32[2,3,192,512]{2,0,1,3:T(2,128)} async-done(((f32[2,3,192,64]{2,0,1,3:T(2,128)}), f32[2,3,192,512]{2,0,1,3:T(2,128)}) %all-gather.2.cloned.1.call-update) | async-done | bytes 2359312 | tf_op jit(solution)/shard_map/all_gather | solution.py:79
  55.2 5.6 %copy.28 = f32[2,3,192,512]{3,2,1,0:T(8,128)} copy(f32[2,3,192,512]{2,0,1,3:T(2,128)} %all-gather.2.cloned.1.call-done) | data formatting | bytes 4718592
  61.8 137.1 %while.19 = (s32[]{:T(128)}, f32[2,3,192,512]{3,2,1,0:T(8,128)S(1)}, f32[2,128,128]{2,1,0:T(8,128)S(1)}, s32[1,1,2]{2,1,0:T(1,128)S(1)}, s32[1,1,2]{2,1,0:T(1,12...) while((s32[]{:T(128)}, ...), condition=%wide.region_1.2_spmd.clone.clone.clone.clone, body=%wide.region_0.1_spmd.clone.clone.clone.clone.sunk | while | flops 2037301248 | bytes 20128300 | solution.py:124
  79.3 1.5 multiply_add_fusion.7
  85.5 1.3 convolution_add_fusion.37
  89.9 1.5 multiply_subtract_fusion.3
  99.0 1.5 add_bitcast_fusion.9
  109.5 1.5 add_bitcast_fusion.10
  120.1 1.5 add_bitcast_fusion.11
  121.8 2.3 dynamic_update_slice.36
  124.3 2.3 dynamic_update_slice.37
  126.7 2.3 dynamic_update_slice.38
  146.8 1.5 multiply_add_fusion.7
  157.0 1.5 multiply_subtract_fusion.3
  166.1 1.5 add_bitcast_fusion.9
  176.7 1.5 add_bitcast_fusion.10
  187.4 1.5 add_bitcast_fusion.11
  189.2 2.3 dynamic_update_slice.36
  191.6 2.3 dynamic_update_slice.37
  194.0 2.3 dynamic_update_slice.38
  199.0 3.4 copy.37
  202.4 6.0 %reshape.42 = f32[512,1152]{1,0:T(8,128)} reshape(f32[512,2,3,192]{3,2,1,0:T(4,128)} %bitcast.367) | data formatting | bytes 4718592
  209.2 41.8 %reduce-scatter.4.cloned.1.call-done = f32[64,1152]{1,0:T(8,128)} async-done(((f32[512,1152]{1,0:T(8,128)}), f32[64,1152]{1,0:T(8,128)}) %reduce-scatter.4.cloned.1.call-update) | async-done | bytes 294928
  250.9 1.3 reshape.43
  252.8 1.3 collective-permute-start.3
  254.1 4.6 %collective-permute-start.2 = (f32[2,3,64,64]{3,2,1,0:T(8,128)S(1)}, f32[2,3,64,64]{3,2,1,0:T(8,128)S(1)}, u32[]{:S(2)}, u32[]{:S(2)}) collective-permute-start(f32[2,3,64,64]{3,2,1,0:T(8,128)S(1)} %copy.40), channel_id=1, source_target_pairs={{0,1},{1,2},{2,3},{4,5},{5,6},{6,7},{8,9},{9,10},{10,11},{12,13},{... | collective-permute-start | bytes 294920 | tf_op jit(solution)/shard_map/ppermute | solution.py:16
  258.6 29.9 %all-reduce.11.cloned.1.call-done = f32[2,128,128]{2,1,0:T(8,128)} async-done(((f32[2,128,128]{2,1,0:T(8,128)}), f32[2,128,128]{2,1,0:T(8,128)}) %all-reduce.11.cloned.1.call-update) | async-done | bytes 131088 | tf_op jit(solution)/shard_map/psum | solution.py:129
  289.4 55.2 %all-reduce.13.cloned.1.call-done = f32[2,128,128]{2,1,0:T(8,128)} async-done(((f32[2,128,128]{2,1,0:T(8,128)}), f32[2,128,128]{2,1,0:T(8,128)}) %all-reduce.13.cloned.1.call-update) | async-done | bytes 131088 | tf_op jit(solution)/shard_map/psum | solution.py:130
  344.6 1.6 copy.56
  (198 shorter events, 96.8 us)
Async XLA Ops:
  7.2 48.1 %all-gather.2.cloned.1.call-start = ((), (), s32[]{:S(2)}) async-start(), calls=%async_computation.1 | async-start | bytes 3538944 | tf_op jit(solution)/shard_map/all_gather | solution.py:79
  8.3 9.9 %collective-permute-start.1 = (f32[2,3,64,64]{2,0,1,3:T(2,128)S(1)}, f32[2,3,64,64]{2,0,1,3:T(2,128)S(1)}, u32[]{:S(2)}, u32[]{:S(2)}) collective-permute-start(f32[2,3,64,64]{2,0,1,3:T(2,128)S(1)} %copy.25), channel_id=1, source_target_pairs={{1,0},{2,1},{3,2},{5,4},{6,5},{7,6},{9,8},{10,9},{11,10},{13,12},{... | collective-permute-start | bytes 294920 | tf_op jit(solution)/shard_map/ppermute | solution.py:18
  9.6 9.7 %collective-permute-start = (f32[2,3,64,64]{2,0,1,3:T(2,128)S(1)}, f32[2,3,64,64]{2,0,1,3:T(2,128)S(1)}, u32[]{:S(2)}, u32[]{:S(2)}) collective-permute-start(f32[2,3,64,64]{2,0,1,3:T(2,128)S(1)} %copy.25), channel_id=1, source_target_pairs={{0,1},{1,2},{2,3},{4,5},{5,6},{6,7},{8,9},{9,10},{10,11},{12,13},{... | collective-permute-start | bytes 294920 | tf_op jit(solution)/shard_map/ppermute | solution.py:16
  20.6 230.3 %reduce-scatter.4.cloned.1.call-start = ((), (), s32[]{:S(2)}) async-start(), calls=%async_computation.4 | async-start | bytes 2654208
  60.8 0.9 copy-start
  60.8 0.9 copy-start.2
  60.8 0.9 copy-start.3
  60.8 0.9 copy-start.4
  60.8 1.0 copy-start.5
  199.0 3.4 copy-start.1
  208.4 80.1 %all-reduce.11.cloned.1.call-start = ((), (), s32[]{:S(2)}) async-start(), calls=%async_computation.2 | async-start | bytes 262144 | tf_op jit(solution)/shard_map/psum | solution.py:129
  209.1 135.5 %all-reduce.13.cloned.1.call-start = ((), (), s32[]{:S(2)}) async-start(), calls=%async_computation.3 | async-start | bytes 262144 | tf_op jit(solution)/shard_map/psum | solution.py:130
  252.8 35.9 %collective-permute-start.3 = (f32[2,3,64,64]{3,2,1,0:T(8,128)S(1)}, f32[2,3,64,64]{3,2,1,0:T(8,128)S(1)}, u32[]{:S(2)}, u32[]{:S(2)}) collective-permute-start(f32[2,3,64,64]{3,2,1,0:T(8,128)S(1)} %copy.41), channel_id=1, source_target_pairs={{1,0},{2,1},{3,2},{5,4},{6,5},{7,6},{9,8},{10,9},{11,10},{13,12},{... | collective-permute-start | bytes 294920 | tf_op jit(solution)/shard_map/ppermute | solution.py:18
  254.1 34.6 %collective-permute-start.2 = (f32[2,3,64,64]{3,2,1,0:T(8,128)S(1)}, f32[2,3,64,64]{3,2,1,0:T(8,128)S(1)}, u32[]{:S(2)}, u32[]{:S(2)}) collective-permute-start(f32[2,3,64,64]{3,2,1,0:T(8,128)S(1)} %copy.40), channel_id=1, source_target_pairs={{0,1},{1,2},{2,3},{4,5},{5,6},{6,7},{8,9},{9,10},{10,11},{12,13},{... | collective-permute-start | bytes 294920 | tf_op jit(solution)/shard_map/ppermute | solution.py:16
Sparse Core Ops, SparseCore 0:
  20.7 34.4 all-gather.1
  208.5 42.3 reduce-scatter.3
  253.8 34.6 all-reduce.10
  291.4 53.1 all-reduce.12
where the time goes:
time: 356 us; the launch traced here: 353 us
  waiting for transfers between devices  166 us (47%)
  matrix products  101 us (28%)
  local copies, waits for them, and re-layouts  36.8 us (10%)
  loops' own time  16.9 us (5%)
  between operations  14.1 us (4%)
  starting transfers between devices  12.9 us (4%)
  other arithmetic  4.94 us (1%)
    dot_general x160, matrix products, matmul(): jnp.dot(first, second, precision=lax.Precision.HIGHEST, preferred_element...  101 us
    psum x1, waiting for transfers between devices, local(): probe_gradient = lax.psum(group_total, 'angle')  55.2 us
    unnamed x5, waiting for transfers between devices  42.5 us
    all_gather x1, waiting for transfers between devices, local(): region = lax.all_gather(framed, 'angle', axis=3, tiled=True)  34.6 us
    psum x1, waiting for transfers between devices, local(): group_total = lax.psum(gradient_probe, 'scan')  29.9 us
    unnamed x21, local copies, waits for them, and re-layouts  20 us
    another operation x1, loops' own time, local(): lax.fori_loop(0, slots, visit, start_carry)  16.9 us
    dynamic_update_slice x6, local copies, waits for them, and re-layouts, visit(): lax.dynamic_update_slice(gradient_region, current + slab_grad[:, k:k + 1]...  13.8 us
  transfers between devices with their start and end apart: 8, of which 6 were waited for; matrix products, arithmetic and copies ran while one was open for 1% of the time, Pallas kernels for 0%

commit v1 on v0

--- a/solution.py
+++ b/solution.py
@@ -126,7 +126,11 @@
     edges = jnp.concatenate([shared[:, :, :band], shared[:, :, 2 * band :]], axis=2)
     rimmed = padded(edges, (("scan", 2),), band)
     object_gradient = shared[:, :, band : 2 * band] + rimmed[:, :, :band] + rimmed[:, :, 3 * band :]
-    group_total = lax.psum(gradient_probe, "scan")
+    group_total = gradient_probe
+    for hop in (1, 2):
+        group_total = group_total + lax.ppermute(
+            group_total, "scan", [(dev, dev ^ hop) for dev in range(4)]
+        )
     probe_gradient = lax.psum(group_total, "angle")
     return (object_gradient, probe_gradient)
 

time: 356 us -> 324 us (0.910)
  waiting for transfers between devices: 166 us -> 129 us
  starting transfers between devices: 12.9 us -> 16.5 us
    psum x1 -> x0, waiting for transfers between devices: 29.9 us -> none  [local(): group_total = lax.psum(gradient_probe, 'scan')]
    unnamed x5 -> x4, waiting for transfers between devices: 42.5 us -> 34.8 us
    psum x1, waiting for transfers between devices: 55.2 us -> 49 us  [local(): probe_gradient = lax.psum(group_total, 'angle')]
    ppermute x0 -> x2, waiting for transfers between devices: none -> 4.06 us  [local(): lax.ppermute(group_total, 'scan', [(dev, dev ^ hop) for dev in range(4)])]
    ppermute x0 -> x2, starting transfers between devices: none -> 3.67 us  [local(): lax.ppermute(group_total, 'scan', [(dev, dev ^ hop) for dev in range(4)])]
    unnamed x21 -> x19, local copies, waits for them, and re-layouts: 20 us -> 20.1 us
  transfers between devices with their start and end apart: 8 -> 9, of which waited for: 6 -> 8; matrix products, arithmetic and copies ran while one was open for 1% -> 1% of each run, Pallas kernels for 0% -> 0%
where the time goes in v1:
time: 324 us; the launch traced here: 321 us
  waiting for transfers between devices  129 us (40%)
  matrix products  101 us (31%)
  local copies, waits for them, and re-layouts  37 us (11%)
  loops' own time  17.5 us (5%)
  starting transfers between devices  16.5 us (5%)
  between operations  14.1 us (4%)
  other arithmetic  5.62 us (2%)
    dot_general x160, matrix products, matmul(): jnp.dot(first, second, precision=lax.Precision.HIGHEST, preferred_element...  101 us
    psum x1, waiting for transfers between devices, local(): probe_gradient = lax.psum(group_total, 'angle')  49 us
    unnamed x4, waiting for transfers between devices  34.8 us
    all_gather x1, waiting for transfers between devices, local(): region = lax.all_gather(framed, 'angle', axis=3, tiled=True)  34.6 us
    unnamed x19, local copies, waits for them, and re-layouts  20.1 us
    another operation x1, loops' own time, local(): lax.fori_loop(0, slots, visit, start_carry)  17.5 us
    dynamic_update_slice x6, local copies, waits for them, and re-layouts, visit(): lax.dynamic_update_slice(gradient_region, current + slab_grad[:, k:k + 1]...  13.8 us
    ppermute x2, starting transfers between devices, padded(): lax.ppermute(tail, axis, [(i, (i + 1) % count) for i in range(ends)])  10.2 us
  transfers between devices with their start and end apart: 9, of which 8 were waited for; matrix products, arithmetic and copies ran while one was open for 1% of the time, Pallas kernels for 0%

profile of v1, /device:TPU:0, one launch (start us, length us, event | category | flops | bytes accessed | tf_op | source)
XLA Modules:
  0.0 321.1 jit_solution(14854042974119993961)
XLA Ops:
  9.6 5.6 %collective-permute-start = (f32[2,3,64,64]{2,0,1,3:T(2,128)S(1)}, f32[2,3,64,64]{2,0,1,3:T(2,128)S(1)}, u32[]{:S(2)}, u32[]{:S(2)}) collective-permute-start(f32[2,3,64,64]{2,0,1,3:T(2,128)S(1)} %copy.25), channel_id=1, source_target_pairs={{0,1},{1,2},{2,3},{4,5},{5,6},{6,7},{8,9},{9,10},{10,11},{12,13},{... | collective-permute-start | bytes 294920 | tf_op jit(solution)/shard_map/ppermute | solution.py:16
  15.2 2.9 collective-permute-done.1
  20.6 34.6 %all-gather.2.cloned.1.call-done = f32[2,3,192,512]{2,0,1,3:T(2,128)} async-done(((f32[2,3,192,64]{2,0,1,3:T(2,128)}), f32[2,3,192,512]{2,0,1,3:T(2,128)}) %all-gather.2.cloned.1.call-update) | async-done | bytes 2359312 | tf_op jit(solution)/shard_map/all_gather | solution.py:79
  55.2 5.6 %copy.28 = f32[2,3,192,512]{3,2,1,0:T(8,128)} copy(f32[2,3,192,512]{2,0,1,3:T(2,128)} %all-gather.2.cloned.1.call-done) | data formatting | bytes 4718592
  61.8 137.8 %while.19 = (s32[]{:T(128)}, f32[2,3,192,512]{3,2,1,0:T(8,128)S(1)}, f32[2,128,128]{2,1,0:T(8,128)S(1)}, s32[1,1,2]{2,1,0:T(1,128)S(1)}, s32[1,1,2]{2,1,0:T(1,12...) while((s32[]{:T(128)}, ...), condition=%wide.region_1.2_spmd.clone.clone.clone.clone, body=%wide.region_0.1_spmd.clone.clone.clone.clone.sunk | while | flops 2037301248 | bytes 20128300 | solution.py:124
  79.6 1.5 multiply_add_fusion.7
  85.9 1.3 convolution_add_fusion.37
  90.2 1.5 multiply_subtract_fusion.3
  99.3 1.5 add_bitcast_fusion.9
  109.8 1.5 add_bitcast_fusion.10
  120.4 1.5 add_bitcast_fusion.11
  122.1 2.3 dynamic_update_slice.36
  124.6 2.3 dynamic_update_slice.37
  127.0 2.3 dynamic_update_slice.38
  147.4 1.5 multiply_add_fusion.7
  157.7 1.5 multiply_subtract_fusion.3
  166.7 1.5 add_bitcast_fusion.9
  177.3 1.5 add_bitcast_fusion.10
  188.1 1.5 add_bitcast_fusion.11
  189.8 2.3 dynamic_update_slice.36
  192.2 2.3 dynamic_update_slice.37
  194.6 2.3 dynamic_update_slice.38
  199.7 3.4 %copy.37 = f32[2,3,192,512]{2,1,0,3:T(4,128)} copy(f32[2,3,192,512]{3,2,1,0:T(8,128)S(1)} %get-tuple-element.508) | data formatting | bytes 4718592
  203.1 6.0 %reshape.42 = f32[512,1152]{1,0:T(8,128)} reshape(f32[512,2,3,192]{3,2,1,0:T(4,128)} %bitcast.367) | data formatting | bytes 4718592
  210.5 4.1 %collective-permute-done.4 = f32[2,128,128]{2,1,0:T(8,128)S(1)} collective-permute-done((f32[2,128,128]{2,1,0:T(8,128)S(1)}, f32[2,128,128]{2,1,0:T(8,128)S(1)}, u32[]{:S(2)}, u32[]{:S(2)}) %collective-permute-start.4) | collective-permute-done | bytes 131104 | tf_op jit(solution)/shard_map/ppermute | solution.py:131
  214.5 2.3 collective-permute-start.5
  216.9 34.8 %reduce-scatter.4.cloned.1.call-done = f32[64,1152]{1,0:T(8,128)} async-done(((f32[512,1152]{1,0:T(8,128)}), f32[64,1152]{1,0:T(8,128)}) %reduce-scatter.4.cloned.1.call-update) | async-done | bytes 294928
  251.6 1.3 reshape.43
  254.8 4.6 %collective-permute-start.2 = (f32[2,3,64,64]{3,2,1,0:T(8,128)S(1)}, f32[2,3,64,64]{3,2,1,0:T(8,128)S(1)}, u32[]{:S(2)}, u32[]{:S(2)}) collective-permute-start(f32[2,3,64,64]{3,2,1,0:T(8,128)S(1)} %copy.40), channel_id=1, source_target_pairs={{0,1},{1,2},{2,3},{4,5},{5,6},{6,7},{8,9},{9,10},{10,11},{12,13},{... | collective-permute-start | bytes 294920 | tf_op jit(solution)/shard_map/ppermute | solution.py:16
  260.2 1.7 collective-permute-done.3
  263.7 49.0 %all-reduce.10.cloned.1.call-done = f32[2,128,128]{2,1,0:T(8,128)} async-done(((f32[2,128,128]{2,1,0:T(8,128)}), f32[2,128,128]{2,1,0:T(8,128)}) %all-reduce.10.cloned.1.call-update) | async-done | bytes 131088 | tf_op jit(solution)/shard_map/psum | solution.py:134
  312.7 1.6 copy.55
  (199 shorter events, 102.0 us)
Async XLA Ops:
  7.2 48.1 %all-gather.2.cloned.1.call-start = ((), (), s32[]{:S(2)}) async-start(), calls=%async_computation.1 | async-start | bytes 3538944 | tf_op jit(solution)/shard_map/all_gather | solution.py:79
  8.3 9.9 %collective-permute-start.1 = (f32[2,3,64,64]{2,0,1,3:T(2,128)S(1)}, f32[2,3,64,64]{2,0,1,3:T(2,128)S(1)}, u32[]{:S(2)}, u32[]{:S(2)}) collective-permute-start(f32[2,3,64,64]{2,0,1,3:T(2,128)S(1)} %copy.25), channel_id=1, source_target_pairs={{1,0},{2,1},{3,2},{5,4},{6,5},{7,6},{9,8},{10,9},{11,10},{13,12},{... | collective-permute-start | bytes 294920 | tf_op jit(solution)/shard_map/ppermute | solution.py:18
  9.6 9.7 %collective-permute-start = (f32[2,3,64,64]{2,0,1,3:T(2,128)S(1)}, f32[2,3,64,64]{2,0,1,3:T(2,128)S(1)}, u32[]{:S(2)}, u32[]{:S(2)}) collective-permute-start(f32[2,3,64,64]{2,0,1,3:T(2,128)S(1)} %copy.25), channel_id=1, source_target_pairs={{0,1},{1,2},{2,3},{4,5},{5,6},{6,7},{8,9},{9,10},{10,11},{12,13},{... | collective-permute-start | bytes 294920 | tf_op jit(solution)/shard_map/ppermute | solution.py:16
  20.6 231.1 %reduce-scatter.4.cloned.1.call-start = ((), (), s32[]{:S(2)}) async-start(), calls=%async_computation.3 | async-start | bytes 2654208
  60.8 0.9 copy-start
  60.8 0.9 copy-start.1
  60.8 0.9 copy-start.2
  60.8 0.9 copy-start.3
  60.8 1.0 copy-start.4
  209.1 103.6 %all-reduce.10.cloned.1.call-start = ((), (), s32[]{:S(2)}) async-start(), calls=%async_computation.2 | async-start | bytes 262144 | tf_op jit(solution)/shard_map/psum | solution.py:134
  209.1 5.4 %collective-permute-start.4 = (f32[2,128,128]{2,1,0:T(8,128)S(1)}, f32[2,128,128]{2,1,0:T(8,128)S(1)}, u32[]{:S(2)}, u32[]{:S(2)}) collective-permute-start(f32[2,128,128]{2,1,0:T(8,128)S(1)} %get-tuple-element.509), channel_id=1, source_target_pairs={{0,1},{1,0},{2,3},{3,2},{4,5},{5,4},{6,7},{7,6},{8,9},{9,8},{10,11... | collective-permute-start | bytes 393224 | tf_op jit(solution)/shard_map/ppermute | solution.py:131
  214.5 44.8 %collective-permute-start.5 = (f32[2,128,128]{2,1,0:T(8,128)S(1)}, f32[2,128,128]{2,1,0:T(8,128)S(1)}, u32[]{:S(2)}, u32[]{:S(2)}) collective-permute-start(f32[2,128,128]{2,1,0:T(8,128)S(1)} %add.635), channel_id=1, source_target_pairs={{0,2},{1,3},{2,0},{3,1},{4,6},{5,7},{6,4},{7,5},{8,10},{9,11},{10,... | collective-permute-start | bytes 393224 | tf_op jit(solution)/shard_map/ppermute | solution.py:131
  253.5 8.4 %collective-permute-start.3 = (f32[2,3,64,64]{3,2,1,0:T(8,128)S(1)}, f32[2,3,64,64]{3,2,1,0:T(8,128)S(1)}, u32[]{:S(2)}, u32[]{:S(2)}) collective-permute-start(f32[2,3,64,64]{3,2,1,0:T(8,128)S(1)} %copy.41), channel_id=1, source_target_pairs={{1,0},{2,1},{3,2},{5,4},{6,5},{7,6},{9,8},{10,9},{11,10},{13,12},{... | collective-permute-start | bytes 294920 | tf_op jit(solution)/shard_map/ppermute | solution.py:18
  254.8 8.3 %collective-permute-start.2 = (f32[2,3,64,64]{3,2,1,0:T(8,128)S(1)}, f32[2,3,64,64]{3,2,1,0:T(8,128)S(1)}, u32[]{:S(2)}, u32[]{:S(2)}) collective-permute-start(f32[2,3,64,64]{3,2,1,0:T(8,128)S(1)} %copy.40), channel_id=1, source_target_pairs={{0,1},{1,2},{2,3},{4,5},{5,6},{6,7},{8,9},{9,10},{10,11},{12,13},{... | collective-permute-start | bytes 294920 | tf_op jit(solution)/shard_map/ppermute | solution.py:16
Sparse Core Ops, SparseCore 0:
  20.7 34.4 all-gather.1
  209.2 42.3 reduce-scatter.3
  260.2 52.5 all-reduce.9
